TPU v7x, 32 devices: a whole 2x2x4 slice. The times are simulated.
32 devices in a mesh: section: 8 (over z, y), fsdp: 4 (over x, core).
Axes of the slice: x: 2, y: 2, z: 4, core: 2. Of those that a mesh axis runs over, the one named last changes fastest.
Arguments:
- source_rows: bfloat16 [3072, 4096], P(('section', 'fsdp')), may hold values from -6 to 6
- target_rows: bfloat16 [1024, 4096], P('section'), may hold values from -6 to 6
- attn_weights: bfloat16 [8, 4, 4096, 3072], P('section', None, None, 'fsdp'), may hold values from -3.76875 to 3.76875
- gains: float32 [8, 4096], P('section'), may hold values from 0.25 to 1.75
- lengths: int32 [8], P('section'), may hold values from 192 to 384
Outputs:
- source_next: bfloat16 [3072, 4096], P(('section', 'fsdp'))
- target_next: bfloat16 [1024, 4096], P('section')
Inputs may be any that keep to these rules, and one draw needn't show every extreme that they name: Keys at positions lengths[s] and beyond are padding.
All inputs are finite; a program needn't handle non-finite values.
Results may differ from a plain program's by a relative error of at most 0.015.
The roundings to bfloat16 on the way count: a program that leaves them out, or rounds other values in their place, can miss the bound.
Values may be sent and summed in bfloat16 or wider, within the bound.
A program may use at most 128 MiB of HBM per device.

v0:
```python
import jax
import jax.numpy as jnp
from jax import lax
from jax.sharding import PartitionSpec as P

HEAD_DIM = 64


def shifted(value, axis, steps):
    count = lax.axis_size(axis)
    pairs = [(source, (source + steps) % count) for source in range(count)]
    return lax.ppermute(value, axis, pairs)


def rms_norm(block_rows, gain_row):
    widened = block_rows.astype(jnp.float32)
    inverse_rms = lax.rsqrt(jnp.mean(widened * widened, axis=-1, keepdims=True) + 1e-06)
    return (widened * inverse_rms * gain_row).astype(jnp.bfloat16)


def project(block_rows, weight):
    return jnp.dot(block_rows, weight, preferred_element_type=jnp.float32).astype(jnp.bfloat16)


def attend(queries, key_rows, values, length):
    query_count = queries.shape[0]
    key_count = key_rows.shape[0]
    head_count = queries.shape[1] // HEAD_DIM
    query_heads = queries.reshape(query_count, head_count, HEAD_DIM)
    key_heads = key_rows.reshape(key_count, head_count, HEAD_DIM)
    value_heads = values.reshape(key_count, head_count, HEAD_DIM)
    scores = (
        jnp.einsum("qhc,khc->hqk", query_heads, key_heads, preferred_element_type=jnp.float32)
        * 0.125
    )
    key_valid = jnp.arange(key_count, dtype=jnp.int32) < length
    scores = jnp.where(key_valid[None, None, :], scores, -1000000000.0)
    row_max = jnp.max(scores, axis=-1, keepdims=True)
    expo = jnp.exp(scores - row_max)
    soft = (expo / jnp.sum(expo, axis=-1, keepdims=True)).astype(jnp.bfloat16)
    context = jnp.einsum("hqk,khc->qhc", soft, value_heads, preferred_element_type=jnp.float32)
    return context.reshape(query_count, head_count * HEAD_DIM).astype(jnp.bfloat16)


def out_partial(context, out_weight):
    return lax.dot_general(
        context, out_weight, (((1,), (1,)), ((), ())), preferred_element_type=jnp.float32
    )


def local(source_rows, target_rows, attn_weights, gains, lengths):
    section_index = lax.axis_index("section")
    encoder_section = section_index < lax.axis_size("section") // 2
    weights = attn_weights[0]
    gain_row = gains[0]
    length = lengths[0]
    source_whole = lax.all_gather(source_rows, "fsdp", axis=0, tiled=True)

    def encoder_work(whole_rows, target_block):
        normed = rms_norm(whole_rows, gain_row)
        context = attend(
            project(normed, weights[0]),
            project(normed, weights[1]),
            project(normed, weights[2]),
            length,
        )
        return (out_partial(context, weights[3]), jnp.zeros(target_block.shape, jnp.float32))

    def decoder_work(whole_rows, target_block):
        normed = rms_norm(target_block, gain_row)
        context = attend(
            project(normed, weights[0]),
            project(whole_rows, weights[1]),
            project(whole_rows, weights[2]),
            length,
        )
        return (jnp.zeros(whole_rows.shape, jnp.float32), out_partial(context, weights[3]))

    source_terms, target_terms = lax.cond(
        encoder_section, encoder_work, decoder_work, source_whole, target_rows
    )
    source_sum = lax.psum_scatter(
        source_terms.astype(jnp.bfloat16), "fsdp", scatter_dimension=0, tiled=True
    ).astype(jnp.float32)
    source_new = (source_rows.astype(jnp.float32) + source_sum).astype(jnp.bfloat16)
    target_sum = lax.psum(target_terms.astype(jnp.bfloat16), "fsdp").astype(jnp.float32)
    target_new = (target_rows.astype(jnp.float32) + target_sum).astype(jnp.bfloat16)
    source_next, target_next = shifted((source_new, target_new), "section", 1)
    return (source_next, target_next)


def solution(mesh):
    in_specs = (
        P(("section", "fsdp"), None),
        P("section", None),
        P("section", None, None, "fsdp"),
        P("section", None),
        P("section"),
    )
    out_specs = (P(("section", "fsdp"), None), P("section", None))
    return jax.shard_map(local, mesh=mesh, in_specs=in_specs, out_specs=out_specs, check_vma=False)
```

profile of v0, /device:TPU:0, one launch (start us, length us, event | category | flops | bytes accessed | tf_op | source)
XLA Modules:
  0.0 194.1 jit_solution(7510881435808563548)
XLA Ops:
  7.2 0.7 all-gather.2.cloned.1.call-update
  7.9 32.8 %all-gather.2.cloned.1.call-done = bf16[384,4096]{1,0:T(8,128)(2,1)} async-done(((bf16[96,4096]{1,0:T(8,128)(2,1)}), bf16[384,4096]{1,0:T(8,128)(2,1)}) %all-gather.2.cloned.1.call-update) | async-done | bytes 3145744 | tf_op jit(solution)/shard_map/all_gather | solution.py:57
  40.8 46.0 %conditional.1 = (bf16[384,4096]{1,0:T(8,128)(2,1)S(1)}, bf16[128,4096]{1,0:T(8,128)(2,1)}) conditional(s32[]{:T(128)} %convert_element_type.82, (bf16[4,4096,768]{2,1,0:T(8,128)(2,1)}, bf16[384,4096]{1,0:T(8,128)(2,1)}, s32[]{:T(128)}, bf16[128,4096]{1,0:T(8,128)(2,1)}, f32[1,4096]{1,0:T(1,128)}) %tuple.31, (bf16[384,4096]{1,0:T(8,128)(2,1)}, ...), branch_computations={%region_0.4_spmd, %region_4.8_spmd} | conditional | flops 10152052736 | bytes 77100880 | solution.py:79
  40.8 2.6 %fusion.39 = f32[384]{0:T(512)S(1)} fusion(bf16[384,4096]{1,0:T(8,128)(2,1)} %get-tuple-element.23), kind=kLoop, calls=%fused_computation.43 | loop fusion | flops 4718208 | bytes 3147264 | tf_op jit(solution)/shard_map/cond/branch_1_fun/reduce_sum | solution.py:17
  43.4 7.4 %fusion.63 = bf16[384,768]{1,0:T(8,128)(2,1)} fusion(bf16[4,4096,768]{2,1,0:T(8,128)(2,1)} %get-tuple-element.25, bf16[384,4096]{1,0:T(8,128)(2,1)} %get-tuple-element.23, f32[4096]{0:T(1024)} %bitcast.73, f32[384]{0:T(512)S(1)} %add_rsqrt_fusion.1), kind=kOutput, calls=%fused_computation.65 | convolution fusion | flops 2422505472 | bytes 10044928 | tf_op jit(solution)/shard_map/cond/branch_1_fun/dot_general | solution.py:22
  50.8 2.1 %copy.18 = bf16[384,768]{0,1:T(8,128)(2,1)} copy(bf16[384,768]{1,0:T(8,128)(2,1)} %fusion.63) | data formatting | bytes 1179648 | tf_op jit(solution)/shard_map/cond/branch_1_fun/convert_element_type | solution.py:22
  52.9 6.3 %fusion.66 = bf16[384,768]{1,0:T(8,128)(2,1)} fusion(bf16[4,4096,768]{2,1,0:T(8,128)(2,1)} %get-tuple-element.25, bf16[384,4096]{1,0:T(8,128)(2,1)S(1)} %copy-done.2, f32[4096]{0:T(1024)S(1)} %bitcast.74, f32[384]{0:T(512)S(1)} %add_rsqrt_fusion.1), kind=kOutput, calls=%fused_computation.66 | convolution fusion | flops 2422505472 | bytes 10044928 | tf_op jit(solution)/shard_map/cond/branch_1_fun/dot_general | solution.py:22
  59.2 2.1 %copy.19 = bf16[384,768]{0,1:T(8,128)(2,1)} copy(bf16[384,768]{1,0:T(8,128)(2,1)} %fusion.66) | data formatting | bytes 1179648 | tf_op jit(solution)/shard_map/cond/branch_1_fun/convert_element_type | solution.py:22
  62.0 7.0 %fusion.77 = (f32[12,384]{1,0:T(8,128)S(1)}, f32[12,384,384]{1,2,0:T(8,128)}) fusion(pred[384]{0:T(512)(128)(4,1)S(1)} %iota_compare_fusion.1, bf16[384,12,64]{0,2,1:T(8,128)(2,1)} %bitcast.64, bf16[384,12,64]{0,2,1:T(8,128)(2,1)} %bitcast.66), kind=kOutput, calls=%fused_computation.75 | convolution fusion | flops 233570688 | bytes 8276352 | tf_op jit(solution)/shard_map/cond/branch_1_fun/sub | solution.py:39
  68.9 6.3 %fusion.60 = bf16[384,768]{1,0:T(8,128)(2,1)} fusion(bf16[4,4096,768]{2,1,0:T(8,128)(2,1)} %get-tuple-element.25, bf16[384,4096]{1,0:T(8,128)(2,1)S(1)} %copy-done.2, f32[4096]{0:T(1024)S(1)} %bitcast.75, f32[384]{0:T(512)S(1)} %add_rsqrt_fusion.1), kind=kOutput, calls=%fused_computation.64 | convolution fusion | flops 2422505472 | bytes 10044928 | tf_op jit(solution)/shard_map/cond/branch_1_fun/dot_general | solution.py:22
  75.2 1.4 copy.17
  76.5 3.7 %fusion.59 = bf16[12,64,384]{2,1,0:T(8,128)(2,1)S(1)} fusion(bf16[384,12,64]{0,2,1:T(8,128)(2,1)S(1)} %bitcast.68, f32[12,384,384]{1,2,0:T(8,128)} %get-tuple-element.36, f32[12,384]{1,0:T(8,128)S(1)} %get-tuple-element.35), kind=kOutput, calls=%fused_computation.63 | convolution fusion | flops 230326272 | bytes 8275968 | tf_op jit(solution)/shard_map/cond/branch_1_fun/hqk,khc->qhc/dot_general | solution.py:41
  80.3 5.4 %fusion.42 = bf16[384,4096]{1,0:T(8,128)(2,1)S(1)} fusion(bf16[384,768]{0,1:T(8,128)(2,1)S(1)} %bitcast.76, bf16[4,4096,768]{2,1,0:T(8,128)(2,1)} %get-tuple-element.25), kind=kOutput, calls=%fused_computation.46 | convolution fusion | flops 2415919104 | bytes 10027008 | tf_op jit(solution)/shard_map/cond/branch_1_fun/dot_general | solution.py:46
  85.7 1.1 broadcast.57
  86.9 1.6 copy-done
  88.5 32.9 %all-reduce.2.cloned.1.call-done = bf16[128,4096]{1,0:T(8,128)(2,1)} async-done(((bf16[128,4096]{1,0:T(8,128)(2,1)}), bf16[128,4096]{1,0:T(8,128)(2,1)}) %all-reduce.2.cloned.1.call-update) | async-done | bytes 1048592 | tf_op jit(solution)/shard_map/psum | solution.py:86
  121.4 1.8 add_convert_fusion
  123.2 1.5 collective-permute-start.1
  124.7 37.6 %reduce-scatter.2.cloned.1.call-done = bf16[96,4096]{1,0:T(8,128)(2,1)} async-done(((bf16[384,4096]{1,0:T(8,128)(2,1)}), bf16[96,4096]{1,0:T(8,128)(2,1)}) %reduce-scatter.2.cloned.1.call-update) | async-done | bytes 786448 | tf_op jit(solution)/shard_map/reduce_scatter | solution.py:82
  162.3 1.6 add_convert_fusion.1
  163.9 1.5 collective-permute-start
  165.4 20.3 %collective-permute-done = bf16[96,4096]{1,0:T(8,128)(2,1)S(1)} collective-permute-done((bf16[96,4096]{1,0:T(8,128)(2,1)S(1)}, bf16[96,4096]{1,0:T(8,128)(2,1)S(1)}, u32[]{:S(2)}, u32[]{:S(2)}) %collective-permute-start) | collective-permute-done | bytes 786464 | tf_op jit(solution)/shard_map/ppermute | solution.py:12
  185.8 0.9 copy.29
  186.6 1.0 copy.30
  (13 shorter events, 0.8 us)
Async XLA Ops:
  7.2 33.6 %all-gather.2.cloned.1.call-start = ((), (), s32[]{:S(2)}) async-start(), calls=%async_computation.1 | async-start | bytes 3932160 | tf_op jit(solution)/shard_map/all_gather | solution.py:57
  7.9 113.5 %all-reduce.2.cloned.1.call-start = ((), (), s32[]{:S(2)}) async-start(), calls=%async_computation.3 | async-start | bytes 2097152 | tf_op jit(solution)/shard_map/psum | solution.py:86
  43.4 9.5 %copy-start.2 = (bf16[384,4096]{1,0:T(8,128)(2,1)S(1)}, bf16[384,4096]{1,0:T(8,128)(2,1)}, u32[]{:S(2)}) copy-start(bf16[384,4096]{1,0:T(8,128)(2,1)} %get-tuple-element.23) | copy-start | bytes 9437188 | tf_op jit(solution)/shard_map/cond
  43.4 9.5 %copy-start.3 = (f32[1,4096]{1,0:T(1,128)S(1)}, f32[1,4096]{1,0:T(1,128)}, u32[]{:S(2)}) copy-start(f32[1,4096]{1,0:T(1,128)} %get-tuple-element.24) | copy-start | bytes 49156 | tf_op jit(solution)/shard_map/cond
  86.8 1.7 copy-start
  86.8 75.5 %reduce-scatter.2.cloned.1.call-start = ((), (), s32[]{:S(2)}) async-start(), calls=%async_computation.2 | async-start | bytes 3932160 | tf_op jit(solution)/shard_map/reduce_scatter | solution.py:82
  123.2 42.2 %collective-permute-start.1 = (bf16[128,4096]{1,0:T(8,128)(2,1)S(1)}, bf16[128,4096]{1,0:T(8,128)(2,1)S(1)}, u32[]{:S(2)}, u32[]{:S(2)}) collective-permute-start(bf16[128,4096]{1,0:T(8,128)(2,1)S(1)} %add_convert_fusion), channel_id=1, source_target_pairs={{0,4},{4,8},{8,12},{12,16},{16,20},{20,24},{24,28},{28,0},{1,5},{5... | collective-permute-start | bytes 3145736 | tf_op jit(solution)/shard_map/ppermute | solution.py:12
  163.9 21.9 %collective-permute-start = (bf16[96,4096]{1,0:T(8,128)(2,1)S(1)}, bf16[96,4096]{1,0:T(8,128)(2,1)S(1)}, u32[]{:S(2)}, u32[]{:S(2)}) collective-permute-start(bf16[96,4096]{1,0:T(8,128)(2,1)S(1)} %add_convert_fusion.1), channel_id=1, source_target_pairs={{0,4},{4,8},{8,12},{12,16},{16,20},{20,24},{24,28},{28,0},{1,5},{5... | collective-permute-start | bytes 2359304 | tf_op jit(solution)/shard_map/ppermute | solution.py:12
Sparse Core Ops, SparseCore 0:
  9.5 31.2 all-gather.1
  86.9 34.4 all-reduce.1
  123.9 38.3 reduce-scatter.1
where the time goes:
time: 195 us; the launch traced here: 194 us
  waiting for transfers between devices  124 us (64%)
  matrix products  36 us (18%)
  between operations  13.8 us (7%)
  local copies, waits for them, and re-layouts  10.1 us (5%)
  other arithmetic  6.59 us (3%)
  starting transfers between devices  3.17 us (2%)
    reduce_scatter x1, waiting for transfers between devices, local(): lax.psum_scatter(source_terms.astype(jnp.bfloat16), 'fsdp', scatter_dimen...  37.6 us
    psum x1, waiting for transfers between devices, local(): lax.psum(target_terms.astype(jnp.bfloat16), 'fsdp').astype(jnp.float32)  32.9 us
    all_gather x1, waiting for transfers between devices, local(): source_whole = lax.all_gather(source_rows, 'fsdp', axis=0, tiled=True)  32.8 us
    ppermute x2, waiting for transfers between devices, shifted(): return lax.ppermute(value, axis, pairs)  20.3 us
    dot_general x3, matrix products, project(): jnp.dot(block_rows, weight, preferred_element_type=jnp.float32)  19.9 us
    sub x1, matrix products, attend(): expo = jnp.exp(scores - row_max)  6.96 us
    convert_element_type x3, local copies, waits for them, and re-layouts, project(): jnp.dot(block_rows, weight, preferred_element_type=jnp.float32)  5.62 us
    dot_general x1, matrix products, out_partial(): lax.dot_general(context, out_weight, (((1,), (1,)), ((), ())), preferred_...  5.45 us
  transfers between devices with their start and end apart: 5, of which 4 were waited for; matrix products, arithmetic and copies ran while one was open for 2% of the time, Pallas kernels for 0%

commit v1 on v0

v1 whole, which is shorter than its diff:
```python
import functools

import jax
import jax.numpy as jnp
from jax import lax
from jax.experimental import pallas as pl
from jax.experimental.pallas import tpu as pltpu
from jax.sharding import PartitionSpec as P

HEAD_DIM = 64
PIECES = 4
F32 = jnp.float32
BF16 = jnp.bfloat16


def row_chunks(rows):
    return 3 if rows % 48 == 0 else 1


def rms_norm(block, gain):
    wide = block.astype(F32)
    inverse = lax.rsqrt(jnp.mean(wide * wide, axis=-1, keepdims=True) + 1e-06)
    return (wide * inverse * gain).astype(BF16)


def kernel(
    n_sec, n_f, x_ref, y_ref, gain_ref, len_ref, w_hbm, so_hbm, to_hbm,
    xs, nb, ny, w, qkv, ctx, term, prt, sums, rem, own, prt_own, fin, sland,
    dterm, dprt, dp, yfin, tland,
    w_sem, l_sem, ag_s, ag_r, pt_s, pt_r, fw_s, fw_r, t1_s, t1_r, x1_s, x1_r,
    t2_s, t2_r, d1_s, d1_r, d2_s, d2_r, ss_s, ss_r, ts_s, ts_r, tf_s, tf_r, o_sem,
):
    chips = n_f // 2
    rows, d = x_ref.shape
    pair = 2 * rows
    total = pair * chips
    t_rows = y_ref.shape[0]
    t_half = t_rows // 2
    width = w.shape[2]
    chunks = row_chunks(rows)
    rc = rows // chunks
    cn = d // PIECES
    sec, f = lax.axis_index("section"), lax.axis_index("fsdp")
    core, chip = lax.rem(f, 2), f // 2
    other = 1 - core
    enc = sec < n_sec // 2
    partner = {"fsdp": chip * 2 + other}
    nxt = {"section": lax.rem(sec + 1, n_sec)}
    prv = {"section": lax.rem(sec + n_sec - 1, n_sec)}

    def ahead(k):
        return lax.rem(chip + k, chips)

    def behind(k):
        return lax.rem(chip + chips - k, chips)

    def peer(h):
        return {"fsdp": h * 2 + core}

    def remote(src, dst, send, recv, dev):
        return pltpu.make_async_remote_copy(
            src_ref=src, dst_ref=dst, send_sem=send, recv_sem=recv,
            device_id=dev, device_id_type=pl.DeviceIdType.MESH,
        )

    def at(start, size):
        return pl.ds(pl.multiple_of(start, 16), size)

    def cols(j):
        return pl.ds(j * cn, cn)

    barrier = pltpu.get_barrier_semaphore()
    greet = [partner, nxt, prv] + [peer(ahead(k)) for k in range(1, chips)]
    for dev in greet:
        pl.semaphore_signal(barrier, inc=1, device_id=dev, device_id_type=pl.DeviceIdType.MESH)

    w_copies = [pltpu.make_async_copy(w_hbm.at[0, i], w.at[i], w_sem.at[i]) for i in range(4)]
    for cp in w_copies:
        cp.start()
    home = pltpu.make_async_copy(x_ref, xs.at[at(f * rows, rows), :], l_sem)
    home.start()
    pl.semaphore_wait(barrier, len(greet))

    def gather_send(k, i):
        return remote(
            x_ref.at[pl.ds(i * rc, rc), :], xs.at[at(f * rows + i * rc, rc), :],
            ag_s.at[k - 1, i], ag_r.at[k - 1, i], peer(ahead(k)),
        )

    def gather_recv(k, i):
        spot = xs.at[at((behind(k) * 2 + core) * rows + i * rc, rc), :]
        return remote(spot, spot, ag_s.at[k - 1, i], ag_r.at[k - 1, i], peer(behind(k)))

    def forward(k, i, which):
        spot = xs.at[at((behind(k) * 2 + which) * rows + i * rc, rc), :]
        return remote(spot, spot, fw_s.at[k - 1, i], fw_r.at[k - 1, i], partner)

    own_rows = xs.at[at(f * rows, rows), :]
    mate_rows = xs.at[at((chip * 2 + other) * rows, rows), :]
    to_partner = remote(x_ref, own_rows, pt_s, pt_r, partner)
    to_partner.start()
    for i in range(chunks):
        for k in range(1, chips):
            gather_send(k, i).start()

    def shift_source(j, src):
        return remote(src.at[:, cols(j)], sland.at[:, cols(j)], ss_s.at[j], ss_r.at[j], nxt)

    def half(which):
        return at(which * t_half, t_half)

    def shift_target(j, src):
        return remote(src, tland.at[half(core), cols(j)], ts_s.at[j], ts_r.at[j], nxt)

    @pl.when(enc)
    def _():
        for j in range(PIECES):
            shift_target(j, y_ref.at[half(core), cols(j)]).start()

    @pl.when(jnp.logical_not(enc))
    def _():
        for j in range(PIECES):
            shift_source(j, x_ref).start()

    gain = gain_ref[...]
    tn = min(width, 256)

    def norm_rows(src, src_start, dst, dst_start, count):
        def step(r, carry):
            dst[at(dst_start + r * 16, 16), :] = rms_norm(src[at(src_start + r * 16, 16), :], gain)
            return carry

        lax.fori_loop(0, count // 16, step, 0)

    def prepare(src_start, dst_start, count):
        @pl.when(enc)
        def _():
            norm_rows(xs, src_start, nb, dst_start, count)

        @pl.when(jnp.logical_not(enc))
        def _():
            def step(r, carry):
                nb[at(dst_start + r * 16, 16), :] = xs[at(src_start + r * 16, 16), :]
                return carry

            lax.fori_loop(0, count // 16, step, 0)

    def project(src, which, start, count):
        def step(t, carry):
            lanes = pl.ds(pl.multiple_of(t * tn, 128), tn)
            qkv[which, at(start, count), lanes] = jnp.dot(
                src[...], w[which, :, lanes], preferred_element_type=F32
            ).astype(BF16)
            return carry

        lax.fori_loop(0, width // tn, step, 0)

    @pl.when(jnp.logical_not(enc))
    def _():
        norm_rows(y_ref, 0, ny, 0, t_rows)

    w_copies[0].wait()

    @pl.when(jnp.logical_not(enc))
    def _():
        project(ny, 0, 0, t_rows)

    for k in range(chips):
        h = behind(k)
        if k == 0:
            home.wait()
            prepare(f * rows, core * rows, rows)
            remote(mate_rows, mate_rows, pt_s, pt_r, partner).wait_recv()
            prepare((chip * 2 + other) * rows, other * rows, rows)
        else:
            for i in range(chunks):
                gather_recv(k, i).wait_recv()
                forward(k, i, core).start()
                prepare((h * 2 + core) * rows + i * rc, core * rows + i * rc, rc)
                forward(k, i, other).wait_recv()
                prepare((h * 2 + other) * rows + i * rc, other * rows + i * rc, rc)

        @pl.when(enc)
        def _():
            project(nb, 0, h * pair, pair)

        for which in (1, 2):
            if k == 0:
                w_copies[which].wait()
            project(nb, which, h * pair, pair)

    length = len_ref[0]

    def attend(start, count):
        key_ok = lax.broadcasted_iota(jnp.int32, (1, total), 1) < length
        first = lax.broadcasted_iota(jnp.int32, (1, 2 * HEAD_DIM), 1) < HEAD_DIM

        def step(t, carry):
            lanes = pl.ds(pl.multiple_of(t * 2 * HEAD_DIM, 128), 2 * HEAD_DIM)
            queries = qkv[0, at(start, count), lanes]
            keys, values = qkv[1, :, lanes], qkv[2, :, lanes]
            outs = []
            for low in (True, False):
                pick = first if low else jnp.logical_not(first)
                masked = queries * jnp.where(pick, 0.125, 0.0).astype(BF16)
                scores = lax.dot_general(
                    masked, keys, (((1,), (1,)), ((), ())), preferred_element_type=F32
                )
                scores = jnp.where(key_ok, scores, -1000000000.0)
                expo = jnp.exp(scores - jnp.max(scores, axis=-1, keepdims=True))
                soft = (expo * (1.0 / jnp.sum(expo, axis=-1, keepdims=True))).astype(BF16)
                outs.append(jnp.dot(soft, values, preferred_element_type=F32))
            ctx[at(start, count), lanes] = jnp.where(first, outs[0], outs[1]).astype(BF16)
            return carry

        lax.fori_loop(0, width // (2 * HEAD_DIM), step, 0)

    on = min(cn, 256)

    def out_piece(start, count, dst, j):
        def step(t, carry):
            lanes = pl.ds(pl.multiple_of(j * cn + t * on, 128), on)
            dst[:, lanes] = lax.dot_general(
                ctx[at(start, count), :], w[3, lanes, :], (((1,), (1,)), ((), ())),
                preferred_element_type=F32,
            ).astype(BF16)
            return carry

        lax.fori_loop(0, cn // on, step, 0)

    def mate_term(k, j):
        return remote(
            term.at[k - 1, at(other * rows, rows), cols(j)], prt.at[k - 1, :, cols(j)],
            t1_s.at[k - 1, j], t1_r.at[k - 1, j], partner,
        )

    def send_sum(k, j):
        return remote(
            sums.at[k - 1, :, cols(j)], rem.at[k - 1, :, cols(j)],
            x1_s.at[k - 1, j], x1_r.at[k - 1, j], peer(ahead(k)),
        )

    def mate_own(j):
        return remote(
            own.at[at(other * rows, rows), cols(j)], prt_own.at[:, cols(j)],
            t2_s.at[j], t2_r.at[j], partner,
        )

    def mate_target(j):
        return remote(
            dterm.at[half(other), cols(j)], dprt.at[:, cols(j)], d1_s.at[j], d1_r.at[j], partner
        )

    def send_target(k, j):
        return remote(
            dp.at[chip, :, cols(j)], dp.at[chip, :, cols(j)],
            d2_s.at[k - 1, j], d2_r.at[k - 1, j], peer(ahead(k)),
        )

    def recv_target(k, j):
        spot = dp.at[behind(k), :, cols(j)]
        return remote(spot, spot, d2_s.at[k - 1, j], d2_r.at[k - 1, j], peer(behind(k)))

    w_copies[3].wait()

    @pl.when(enc)
    def _():
        for k in range(1, chips):
            start = ahead(k) * pair
            attend(start, pair)

            def pass_on(j):
                mate_term(k, j).wait_recv()
                mine = term[k - 1, at(core * rows, rows), cols(j)].astype(F32)
                sums[k - 1, :, cols(j)] = (mine + prt[k - 1, :, cols(j)].astype(F32)).astype(BF16)
                send_sum(k, j).start()

            for j in range(PIECES):
                out_piece(start, pair, term.at[k - 1], j)
                mate_term(k, j).start()
                if j:
                    pass_on(j - 1)
            pass_on(PIECES - 1)
        attend(chip * pair, pair)
        for j in range(PIECES):
            out_piece(chip * pair, pair, own, j)
            mate_own(j).start()
        for j in range(PIECES):
            mate_own(j).wait_recv()
            delta = own[at(core * rows, rows), cols(j)].astype(F32) + prt_own[:, cols(j)].astype(F32)
            for k in range(1, chips):
                send_sum(k, j).wait_recv()
                delta += rem[k - 1, :, cols(j)].astype(F32)
            fin[:, cols(j)] = (x_ref[:, cols(j)].astype(F32) + delta).astype(BF16)
            shift_source(j, fin).start()
        for j in range(PIECES):
            mate_own(j).wait_send()
            for k in range(1, chips):
                mate_term(k, j).wait_send()
                send_sum(k, j).wait_send()

    @pl.when(jnp.logical_not(enc))
    def _():
        attend(0, t_rows)

        def pass_on(j):
            mate_target(j).wait_recv()
            mine = dterm[half(core), cols(j)].astype(F32)
            dp[chip, :, cols(j)] = (mine + dprt[:, cols(j)].astype(F32)).astype(BF16)
            for k in range(1, chips):
                send_target(k, j).start()

        for j in range(PIECES):
            out_piece(0, t_rows, dterm, j)
            mate_target(j).start()
            if j:
                pass_on(j - 1)
        pass_on(PIECES - 1)
        for j in range(PIECES):
            for k in range(1, chips):
                recv_target(k, j).wait_recv()
            delta = dp[0, :, cols(j)].astype(F32)
            for h in range(1, chips):
                delta += dp[h, :, cols(j)].astype(F32)
            yfin[:, cols(j)] = (y_ref[half(core), cols(j)].astype(F32) + delta).astype(BF16)
            shift_target(j, yfin.at[:, cols(j)]).start()
        for j in range(PIECES):
            mate_target(j).wait_send()
            for k in range(1, chips):
                send_target(k, j).wait_send()

    def cross(j, which):
        spot = tland.at[half(which), cols(j)]
        return remote(spot, spot, tf_s.at[j], tf_r.at[j], partner)

    def put_target(j, which, slot):
        return pltpu.make_async_copy(
            tland.at[half(which), cols(j)], to_hbm.at[half(which), cols(j)], o_sem.at[slot, j]
        )

    def put_source(j):
        return pltpu.make_async_copy(sland.at[:, cols(j)], so_hbm.at[:, cols(j)], o_sem.at[2, j])

    for j in range(PIECES):
        shift_target(j, yfin.at[:, cols(j)]).wait_recv()
        cross(j, core).start()
        put_target(j, core, 0).start()
    for j in range(PIECES):
        shift_source(j, fin).wait_recv()
        put_source(j).start()
    for j in range(PIECES):
        cross(j, other).wait_recv()
        put_target(j, other, 1).start()

    to_partner.wait_send()
    for i in range(chunks):
        for k in range(1, chips):
            gather_send(k, i).wait_send()
            forward(k, i, core).wait_send()
    for j in range(PIECES):
        shift_source(j, fin).wait_send()
        shift_target(j, yfin.at[:, cols(j)]).wait_send()
        cross(j, core).wait_send()
        put_target(j, core, 0).wait()
        put_target(j, other, 1).wait()
        put_source(j).wait()


def local(n_sec, n_f, source_rows, target_rows, attn_weights, gains, lengths):
    chips = n_f // 2
    more = max(chips - 1, 1)
    rows, d = source_rows.shape
    t_rows = target_rows.shape[0]
    width = attn_weights.shape[3]
    pair, total, t_half = 2 * rows, rows * n_f, t_rows // 2
    chunks = row_chunks(rows)
    q_rows = max(total, t_rows)
    dma = pltpu.SemaphoreType.DMA
    vmem = lambda *shape: pltpu.VMEM(shape, BF16)
    scratch = [
        vmem(total, d), vmem(pair, d), vmem(t_rows, d), vmem(4, d, width),
        vmem(3, q_rows, width), vmem(q_rows, width),
        vmem(more, pair, d), vmem(more, rows, d), vmem(more, rows, d), vmem(more, rows, d),
        vmem(pair, d), vmem(rows, d), vmem(rows, d), vmem(rows, d),
        vmem(t_rows, d), vmem(t_half, d), vmem(chips, t_half, d), vmem(t_half, d), vmem(t_rows, d),
        dma((4,)), dma, dma((more, chunks)), dma((more, chunks)), dma, dma,
        dma((more, chunks)), dma((more, chunks)),
        dma((more, PIECES)), dma((more, PIECES)), dma((more, PIECES)), dma((more, PIECES)),
        dma((PIECES,)), dma((PIECES,)), dma((PIECES,)), dma((PIECES,)),
        dma((more, PIECES)), dma((more, PIECES)),
        dma((PIECES,)), dma((PIECES,)), dma((PIECES,)), dma((PIECES,)), dma((PIECES,)), dma((PIECES,)),
        dma((3, PIECES)),
    ]
    in_vmem = pl.BlockSpec(memory_space=pltpu.VMEM)
    anywhere = pl.BlockSpec(memory_space=pl.ANY)
    return pl.pallas_call(
        functools.partial(kernel, n_sec, n_f),
        out_shape=(
            jax.ShapeDtypeStruct(source_rows.shape, BF16),
            jax.ShapeDtypeStruct(target_rows.shape, BF16),
        ),
        in_specs=[in_vmem, in_vmem, in_vmem, pl.BlockSpec(memory_space=pltpu.SMEM), anywhere],
        out_specs=(anywhere, anywhere),
        scratch_shapes=scratch,
        compiler_params=pltpu.CompilerParams(
            collective_id=0, has_side_effects=True, vmem_limit_bytes=60 * 1024 * 1024
        ),
    )(source_rows, target_rows, gains, lengths, attn_weights)


def solution(mesh):
    in_specs = (
        P(("section", "fsdp"), None),
        P("section", None),
        P("section", None, None, "fsdp"),
        P("section", None),
        P("section"),
    )
    out_specs = (P(("section", "fsdp"), None), P("section", None))
    body = functools.partial(local, mesh.shape["section"], mesh.shape["fsdp"])
    return jax.shard_map(body, mesh=mesh, in_specs=in_specs, out_specs=out_specs, check_vma=False)
```

time: 195 us -> 79.6 us (0.41)
  waiting for transfers between devices: 124 us -> 0 us
  Pallas kernels: 0 us -> 73.4 us
  matrix products: 36 us -> 0 us
  between operations: 13.8 us -> 1.29 us
  other arithmetic: 6.59 us -> 0 us
  local copies, waits for them, and re-layouts: 10.1 us -> 4.35 us
  starting transfers between devices: 3.17 us -> 0 us
    pallas_call x0 -> x1, Pallas kernels: none -> 73.4 us  [local(): pl.pallas_call(functools.partial(kernel, n_sec, n_f), out_shape=(jax.Shap...]
    reduce_scatter x1 -> x0, waiting for transfers between devices: 37.6 us -> none  [local(): lax.psum_scatter(source_terms.astype(jnp.bfloat16), 'fsdp', scatter_dimen...]
    psum x1 -> x0, waiting for transfers between devices: 32.9 us -> none  [local(): lax.psum(target_terms.astype(jnp.bfloat16), 'fsdp').astype(jnp.float32)]
    all_gather x1 -> x0, waiting for transfers between devices: 32.8 us -> none  [local(): source_whole = lax.all_gather(source_rows, 'fsdp', axis=0, tiled=True)]
    dot_general x5 -> x0, matrix products: 29 us -> none  [the longest x3 19.9 us: project(): jnp.dot(block_rows, weight, preferred_element_type=jnp.float32)]
    ppermute x2 -> x0, waiting for transfers between devices: 20.3 us -> none  [shifted(): return lax.ppermute(value, axis, pairs)]
    sub x1 -> x0, matrix products: 6.96 us -> none  [attend(): expo = jnp.exp(scores - row_max)]
    convert_element_type x3 -> x0, local copies, waits for them, and re-layouts: 5.62 us -> none  [project(): jnp.dot(block_rows, weight, preferred_element_type=jnp.float32)]
  transfers between devices with their start and end apart: 5 -> 0, of which waited for: 4 -> 0; matrix products, arithmetic and copies ran while one was open for 2% -> 0% of each run, Pallas kernels for 0% -> 0%
where the time goes in v1:
time: 79.6 us; the launch traced here: 79 us
  Pallas kernels  73.4 us (92%)
  local copies, waits for them, and re-layouts  4.35 us (5%)
  between operations  1.29 us (2%)
    pallas_call x1, Pallas kernels, local(): pl.pallas_call(functools.partial(kernel, n_sec, n_f), out_shape=(jax.Shap...  73.4 us
    unnamed x2, local copies, waits for them, and re-layouts  4.35 us

profile of v1, /device:TPU:0, one launch (start us, length us, event | category | flops | bytes accessed | tf_op | source)
XLA Modules:
  0.0 79.0 jit_solution(7769799773850318817)
XLA Ops:
  1.3 73.4 %shard_map.68 = (bf16[96,4096]{1,0:T(8,128)(2,1)}, bf16[128,4096]{1,0:T(8,128)(2,1)}) custom-call(bf16[96,4096]{1,0:T(8,128)(2,1)} %x_ref.1, bf16[128,4096]{1,0:T(8,128)(2,1)} %y_ref.1, f32[1,4096]{1,0:T(1,128)} %gain_ref.1, s32[1]{0:T(128)S(6)} %copy.9.len_ref, bf16[1,4,4096,768]{3,2,1,0:T(8,128)(2,1)} %w_hbm.1), custom_call_target="tpu_custom_call" | custom-call | tf_op jit(solution)/shard_map/pallas_call | solution.py:396
  74.6 2.1 %copy.10 = bf16[96,4096]{1,0:T(8,128)(2,1)} copy(bf16[96,4096]{1,0:T(8,128)(2,1)} %get-tuple-element.4) | data formatting | bytes 1572864
  76.7 2.3 %copy.11 = bf16[128,4096]{1,0:T(8,128)(2,1)} copy(bf16[128,4096]{1,0:T(8,128)(2,1)} %get-tuple-element.5) | data formatting | bytes 2097152

commit v2 on v1

--- a/solution.py
+++ b/solution.py
@@ -8,13 +8,10 @@
 from jax.sharding import PartitionSpec as P
 
 HEAD_DIM = 64
-PIECES = 4
+PIECES = 8
+GATHER = 8
 F32 = jnp.float32
 BF16 = jnp.bfloat16
-
-
-def row_chunks(rows):
-    return 3 if rows % 48 == 0 else 1
 
 
 def rms_norm(block, gain):
@@ -25,9 +22,9 @@
 
 def kernel(
     n_sec, n_f, x_ref, y_ref, gain_ref, len_ref, w_hbm, so_hbm, to_hbm,
-    xs, nb, ny, w, qkv, ctx, term, prt, sums, rem, own, prt_own, fin, sland,
+    xs, ny, w, acc, qkv, ctx, term, prt, sums, rem, own, prt_own, fin, sland,
     dterm, dprt, dp, yfin, tland,
-    w_sem, l_sem, ag_s, ag_r, pt_s, pt_r, fw_s, fw_r, t1_s, t1_r, x1_s, x1_r,
+    w_sem, ag_s, ag_r, pt_s, pt_r, fw_s, fw_r, t1_s, t1_r, x1_s, x1_r,
     t2_s, t2_r, d1_s, d1_r, d2_s, d2_r, ss_s, ss_r, ts_s, ts_r, tf_s, tf_r, o_sem,
 ):
     chips = n_f // 2
@@ -37,9 +34,7 @@
     t_rows = y_ref.shape[0]
     t_half = t_rows // 2
     width = w.shape[2]
-    chunks = row_chunks(rows)
-    rc = rows // chunks
-    cn = d // PIECES
+    cn, gn = d // PIECES, d // GATHER
     sec, f = lax.axis_index("section"), lax.axis_index("fsdp")
     core, chip = lax.rem(f, 2), f // 2
     other = 1 - core
@@ -77,31 +72,50 @@
     w_copies = [pltpu.make_async_copy(w_hbm.at[0, i], w.at[i], w_sem.at[i]) for i in range(4)]
     for cp in w_copies:
         cp.start()
-    home = pltpu.make_async_copy(x_ref, xs.at[at(f * rows, rows), :], l_sem)
-    home.start()
+    gain = gain_ref[...]
+
+    def norm_rows(src, dst, dst_start, count):
+        size = 32 if count % 32 == 0 else 16
+
+        def step(r, carry):
+            dst[at(dst_start + r * size, size), :] = rms_norm(src[at(r * size, size), :], gain)
+            return carry
+
+        lax.fori_loop(0, count // size, step, 0)
+
+    @pl.when(enc)
+    def _():
+        norm_rows(x_ref, xs, f * rows, rows)
+
+    @pl.when(jnp.logical_not(enc))
+    def _():
+        xs[at(f * rows, rows), :] = x_ref[...]
+
     pl.semaphore_wait(barrier, len(greet))
 
-    def gather_send(k, i):
-        return remote(
-            x_ref.at[pl.ds(i * rc, rc), :], xs.at[at(f * rows + i * rc, rc), :],
-            ag_s.at[k - 1, i], ag_r.at[k - 1, i], peer(ahead(k)),
-        )
-
-    def gather_recv(k, i):
-        spot = xs.at[at((behind(k) * 2 + core) * rows + i * rc, rc), :]
-        return remote(spot, spot, ag_s.at[k - 1, i], ag_r.at[k - 1, i], peer(behind(k)))
-
-    def forward(k, i, which):
-        spot = xs.at[at((behind(k) * 2 + which) * rows + i * rc, rc), :]
-        return remote(spot, spot, fw_s.at[k - 1, i], fw_r.at[k - 1, i], partner)
-
-    own_rows = xs.at[at(f * rows, rows), :]
-    mate_rows = xs.at[at((chip * 2 + other) * rows, rows), :]
-    to_partner = remote(x_ref, own_rows, pt_s, pt_r, partner)
-    to_partner.start()
-    for i in range(chunks):
+    def block(h, which):
+        return at((h * 2 + which) * rows, rows)
+
+    def gather_send(k, j):
+        spot = xs.at[block(chip, core), pl.ds(j * gn, gn)]
+        return remote(spot, spot, ag_s.at[k - 1, j], ag_r.at[k - 1, j], peer(ahead(k)))
+
+    def gather_recv(k, j):
+        spot = xs.at[block(behind(k), core), pl.ds(j * gn, gn)]
+        return remote(spot, spot, ag_s.at[k - 1, j], ag_r.at[k - 1, j], peer(behind(k)))
+
+    def forward(k, j, which):
+        spot = xs.at[block(behind(k), which), pl.ds(j * gn, gn)]
+        return remote(spot, spot, fw_s.at[k - 1, j], fw_r.at[k - 1, j], partner)
+
+    def swap(which):
+        spot = xs.at[block(chip, which), :]
+        return remote(spot, spot, pt_s, pt_r, partner)
+
+    for j in range(GATHER):
         for k in range(1, chips):
-            gather_send(k, i).start()
+            gather_send(k, j).start()
+    swap(core).start()
 
     def shift_source(j, src):
         return remote(src.at[:, cols(j)], sland.at[:, cols(j)], ss_s.at[j], ss_r.at[j], nxt)
@@ -122,72 +136,55 @@
         for j in range(PIECES):
             shift_source(j, x_ref).start()
 
-    gain = gain_ref[...]
-    tn = min(width, 256)
-
-    def norm_rows(src, src_start, dst, dst_start, count):
-        def step(r, carry):
-            dst[at(dst_start + r * 16, 16), :] = rms_norm(src[at(src_start + r * 16, 16), :], gain)
-            return carry
-
-        lax.fori_loop(0, count // 16, step, 0)
-
-    def prepare(src_start, dst_start, count):
-        @pl.when(enc)
-        def _():
-            norm_rows(xs, src_start, nb, dst_start, count)
-
-        @pl.when(jnp.logical_not(enc))
-        def _():
-            def step(r, carry):
-                nb[at(dst_start + r * 16, 16), :] = xs[at(src_start + r * 16, 16), :]
-                return carry
-
-            lax.fori_loop(0, count // 16, step, 0)
-
     def project(src, which, start, count):
-        def step(t, carry):
-            lanes = pl.ds(pl.multiple_of(t * tn, 128), tn)
-            qkv[which, at(start, count), lanes] = jnp.dot(
-                src[...], w[which, :, lanes], preferred_element_type=F32
-            ).astype(BF16)
-            return carry
-
-        lax.fori_loop(0, width // tn, step, 0)
+        qkv[which, at(start, count), :] = jnp.dot(
+            src, w[which], preferred_element_type=F32
+        ).astype(BF16)
+
+    def project_piece(which, h, j):
+        part = jnp.dot(
+            xs[at(h * pair, pair), pl.ds(j * gn, gn)], w[which, pl.ds(j * gn, gn), :],
+            preferred_element_type=F32,
+        )
+        if j:
+            part = part + acc[which]
+        if j < GATHER - 1:
+            acc[which] = part
+        else:
+            qkv[which, at(h * pair, pair), :] = part.astype(BF16)
 
     @pl.when(jnp.logical_not(enc))
     def _():
-        norm_rows(y_ref, 0, ny, 0, t_rows)
+        norm_rows(y_ref, ny, 0, t_rows)
 
     w_copies[0].wait()
 
     @pl.when(jnp.logical_not(enc))
     def _():
-        project(ny, 0, 0, t_rows)
-
-    for k in range(chips):
-        h = behind(k)
-        if k == 0:
-            home.wait()
-            prepare(f * rows, core * rows, rows)
-            remote(mate_rows, mate_rows, pt_s, pt_r, partner).wait_recv()
-            prepare((chip * 2 + other) * rows, other * rows, rows)
-        else:
-            for i in range(chunks):
-                gather_recv(k, i).wait_recv()
-                forward(k, i, core).start()
-                prepare((h * 2 + core) * rows + i * rc, core * rows + i * rc, rc)
-                forward(k, i, other).wait_recv()
-                prepare((h * 2 + other) * rows + i * rc, other * rows + i * rc, rc)
-
-        @pl.when(enc)
-        def _():
-            project(nb, 0, h * pair, pair)
-
-        for which in (1, 2):
-            if k == 0:
-                w_copies[which].wait()
-            project(nb, which, h * pair, pair)
+        project(ny[...], 0, 0, t_rows)
+
+    swap(other).wait_recv()
+
+    @pl.when(enc)
+    def _():
+        project(xs[at(chip * pair, pair), :], 0, chip * pair, pair)
+
+    for which in (1, 2):
+        w_copies[which].wait()
+        project(xs[at(chip * pair, pair), :], which, chip * pair, pair)
+
+    for k in range(1, chips):
+        for j in range(GATHER):
+            gather_recv(k, j).wait_recv()
+            forward(k, j, core).start()
+            forward(k, j, other).wait_recv()
+
+            @pl.when(enc)
+            def _():
+                project_piece(0, behind(k), j)
+
+            project_piece(1, behind(k), j)
+            project_piece(2, behind(k), j)
 
     length = len_ref[0]
 
@@ -198,24 +195,25 @@
         def step(t, carry):
             lanes = pl.ds(pl.multiple_of(t * 2 * HEAD_DIM, 128), 2 * HEAD_DIM)
             queries = qkv[0, at(start, count), lanes]
-            keys, values = qkv[1, :, lanes], qkv[2, :, lanes]
-            outs = []
-            for low in (True, False):
-                pick = first if low else jnp.logical_not(first)
-                masked = queries * jnp.where(pick, 0.125, 0.0).astype(BF16)
-                scores = lax.dot_general(
-                    masked, keys, (((1,), (1,)), ((), ())), preferred_element_type=F32
-                )
-                scores = jnp.where(key_ok, scores, -1000000000.0)
-                expo = jnp.exp(scores - jnp.max(scores, axis=-1, keepdims=True))
-                soft = (expo * (1.0 / jnp.sum(expo, axis=-1, keepdims=True))).astype(BF16)
-                outs.append(jnp.dot(soft, values, preferred_element_type=F32))
-            ctx[at(start, count), lanes] = jnp.where(first, outs[0], outs[1]).astype(BF16)
+            keys, values = qkv[1, :total, lanes], qkv[2, :total, lanes]
+            low = queries * jnp.where(first, 0.125, 0.0).astype(BF16)
+            high = queries * jnp.where(first, 0.0, 0.125).astype(BF16)
+            scores = lax.dot_general(
+                jnp.concatenate([low, high], axis=0), keys, (((1,), (1,)), ((), ())),
+                preferred_element_type=F32,
+            )
+            scores = jnp.where(key_ok, scores, -1000000000.0)
+            expo = jnp.exp(scores - jnp.max(scores, axis=-1, keepdims=True))
+            soft = (expo * (1.0 / jnp.sum(expo, axis=-1, keepdims=True))).astype(BF16)
+            mixed = jnp.dot(soft, values, preferred_element_type=F32)
+            ctx[at(start, count), lanes] = jnp.where(
+                first, mixed[:count], mixed[count:]
+            ).astype(BF16)
             return carry
 
         lax.fori_loop(0, width // (2 * HEAD_DIM), step, 0)
 
-    on = min(cn, 256)
+    on = min(cn, 1024)
 
     def out_piece(start, count, dst, j):
         def step(t, carry):
@@ -352,11 +350,11 @@
         cross(j, other).wait_recv()
         put_target(j, other, 1).start()
 
-    to_partner.wait_send()
-    for i in range(chunks):
+    swap(core).wait_send()
+    for j in range(GATHER):
         for k in range(1, chips):
-            gather_send(k, i).wait_send()
-            forward(k, i, core).wait_send()
+            gather_send(k, j).wait_send()
+            forward(k, j, core).wait_send()
     for j in range(PIECES):
         shift_source(j, fin).wait_send()
         shift_target(j, yfin.at[:, cols(j)]).wait_send()
@@ -373,18 +371,17 @@
     t_rows = target_rows.shape[0]
     width = attn_weights.shape[3]
     pair, total, t_half = 2 * rows, rows * n_f, t_rows // 2
-    chunks = row_chunks(rows)
     q_rows = max(total, t_rows)
     dma = pltpu.SemaphoreType.DMA
     vmem = lambda *shape: pltpu.VMEM(shape, BF16)
     scratch = [
-        vmem(total, d), vmem(pair, d), vmem(t_rows, d), vmem(4, d, width),
+        vmem(total, d), vmem(t_rows, d), vmem(4, d, width), pltpu.VMEM((3, pair, width), F32),
         vmem(3, q_rows, width), vmem(q_rows, width),
         vmem(more, pair, d), vmem(more, rows, d), vmem(more, rows, d), vmem(more, rows, d),
         vmem(pair, d), vmem(rows, d), vmem(rows, d), vmem(rows, d),
         vmem(t_rows, d), vmem(t_half, d), vmem(chips, t_half, d), vmem(t_half, d), vmem(t_rows, d),
-        dma((4,)), dma, dma((more, chunks)), dma((more, chunks)), dma, dma,
-        dma((more, chunks)), dma((more, chunks)),
+        dma((4,)), dma((more, GATHER)), dma((more, GATHER)), dma, dma,
+        dma((more, GATHER)), dma((more, GATHER)),
         dma((more, PIECES)), dma((more, PIECES)), dma((more, PIECES)), dma((more, PIECES)),
         dma((PIECES,)), dma((PIECES,)), dma((PIECES,)), dma((PIECES,)),
         dma((more, PIECES)), dma((more, PIECES)),

time: 79.6 us -> 72.2 us (0.907)
  Pallas kernels: 73.4 us -> 65.8 us
    pallas_call x1, Pallas kernels: 73.4 us -> 65.8 us  [local(): pl.pallas_call(functools.partial(kernel, n_sec, n_f), out_shape=(jax.Shap...]
where the time goes in v2:
time: 72.2 us; the launch traced here: 71.4 us
  Pallas kernels  65.8 us (91%)
  local copies, waits for them, and re-layouts  4.35 us (6%)
  between operations  1.29 us (2%)
    pallas_call x1, Pallas kernels, local(): pl.pallas_call(functools.partial(kernel, n_sec, n_f), out_shape=(jax.Shap...  65.8 us
    unnamed x2, local copies, waits for them, and re-layouts  4.35 us

profile of v2, /device:TPU:0, one launch (start us, length us, event | category | flops | bytes accessed | tf_op | source)
XLA Modules:
  0.0 71.4 jit_solution(13331337611714750300)
XLA Ops:
  1.3 65.8 %shard_map.68 = (bf16[96,4096]{1,0:T(8,128)(2,1)}, bf16[128,4096]{1,0:T(8,128)(2,1)}) custom-call(bf16[96,4096]{1,0:T(8,128)(2,1)} %x_ref.1, bf16[128,4096]{1,0:T(8,128)(2,1)} %y_ref.1, f32[1,4096]{1,0:T(1,128)} %gain_ref.1, s32[1]{0:T(128)S(6)} %copy.9.len_ref, bf16[1,4,4096,768]{3,2,1,0:T(8,128)(2,1)} %w_hbm.1), custom_call_target="tpu_custom_call" | custom-call | tf_op jit(solution)/shard_map/pallas_call | solution.py:393
  67.0 2.1 %copy.10 = bf16[96,4096]{1,0:T(8,128)(2,1)} copy(bf16[96,4096]{1,0:T(8,128)(2,1)} %get-tuple-element.4) | data formatting | bytes 1572864
  69.1 2.3 %copy.11 = bf16[128,4096]{1,0:T(8,128)(2,1)} copy(bf16[128,4096]{1,0:T(8,128)(2,1)} %get-tuple-element.5) | data formatting | bytes 2097152

commit v3 on v2

--- a/solution.py
+++ b/solution.py
@@ -8,8 +8,8 @@
 from jax.sharding import PartitionSpec as P
 
 HEAD_DIM = 64
-PIECES = 8
-GATHER = 8
+PIECES = 4
+GATHER = 4
 F32 = jnp.float32
 BF16 = jnp.bfloat16
 
@@ -390,19 +390,54 @@
     ]
     in_vmem = pl.BlockSpec(memory_space=pltpu.VMEM)
     anywhere = pl.BlockSpec(memory_space=pl.ANY)
-    return pl.pallas_call(
+    moved = pl.pallas_call(
         functools.partial(kernel, n_sec, n_f),
         out_shape=(
-            jax.ShapeDtypeStruct(source_rows.shape, BF16),
-            jax.ShapeDtypeStruct(target_rows.shape, BF16),
+            pltpu.VMEM(source_rows.shape, BF16),
+            pltpu.VMEM(target_rows.shape, BF16),
         ),
         in_specs=[in_vmem, in_vmem, in_vmem, pl.BlockSpec(memory_space=pltpu.SMEM), anywhere],
         out_specs=(anywhere, anywhere),
         scratch_shapes=scratch,
         compiler_params=pltpu.CompilerParams(
-            collective_id=0, has_side_effects=True, vmem_limit_bytes=60 * 1024 * 1024
+            collective_id=0, has_side_effects=True, vmem_limit_bytes=52 * 1024 * 1024
         ),
     )(source_rows, target_rows, gains, lengths, attn_weights)
+    return settle(*moved)
+
+
+def settle(source, target):
+    def body(a_ref, b_ref, a_out, b_out, a_vmem, b_vmem, in_sem, out_sem):
+        plan = []
+        for src, mid, dst in ((a_ref, a_vmem, a_out), (b_ref, b_vmem, b_out)):
+            step = src.shape[1] // 4
+            for j in range(4):
+                lanes = pl.ds(j * step, step)
+                n = len(plan)
+                plan.append((
+                    pltpu.make_async_copy(src.at[:, lanes], mid.at[:, lanes], in_sem.at[n]),
+                    pltpu.make_async_copy(mid.at[:, lanes], dst.at[:, lanes], out_sem.at[n]),
+                ))
+        for into, _ in plan:
+            into.start()
+        for into, out in plan:
+            into.wait()
+            out.start()
+        for _, out in plan:
+            out.wait()
+
+    anywhere = pl.BlockSpec(memory_space=pl.ANY)
+    return pl.pallas_call(
+        body,
+        out_shape=tuple(jax.ShapeDtypeStruct(v.shape, v.dtype) for v in (source, target)),
+        in_specs=[anywhere, anywhere],
+        out_specs=(anywhere, anywhere),
+        scratch_shapes=[
+            pltpu.VMEM(source.shape, source.dtype), pltpu.VMEM(target.shape, target.dtype),
+            pltpu.SemaphoreType.DMA((8,)), pltpu.SemaphoreType.DMA((8,)),
+        ],
+        compiler_params=pltpu.CompilerParams(vmem_limit_bytes=8 * 1024 * 1024),
+    )(source, target)
 
 
 def solution(mesh):

time: 72.2 us -> 65.7 us (0.910)
  local copies, waits for them, and re-layouts: 4.35 us -> 0.71 us
  Pallas kernels: 65.8 us -> 63.3 us
    unnamed x2, local copies, waits for them, and re-layouts: 4.35 us -> 0.71 us
    pallas_call x1 -> x2, Pallas kernels: 65.8 us -> 63.3 us  [the longest x1 61.7 us: local(): pl.pallas_call(functools.partial(kernel, n_sec, n_f), out_shape=(pltpu.VM...]
where the time goes in v3:
time: 65.7 us; the launch traced here: 65.4 us
  Pallas kernels  63.3 us (96%)
  between operations  1.45 us (2%)
  local copies, waits for them, and re-layouts  0.71 us (1%)
    pallas_call x1, Pallas kernels, local(): pl.pallas_call(functools.partial(kernel, n_sec, n_f), out_shape=(pltpu.VM...  61.7 us
    pallas_call x1, Pallas kernels, settle(): pl.pallas_call(body, out_shape=tuple((jax.ShapeDtypeStruct(v.shape, v.dty...  1.55 us

profile of v3, /device:TPU:0, one launch (start us, length us, event | category | flops | bytes accessed | tf_op | source)
XLA Modules:
  0.0 65.4 jit_solution(12141543550491116032)
XLA Ops:
  1.3 0.0 copy-start
  1.3 0.7 %copy-done = f32[1,4096]{1,0:T(1,128)S(1)} copy-done((f32[1,4096]{1,0:T(1,128)S(1)}, f32[1,4096]{1,0:T(1,128)}, u32[]{:S(2)}) %copy-start) | copy-done | bytes 16408
  2.0 61.7 %shard_map.68 = (bf16[96,4096]{1,0:T(8,128)(2,1)S(1)}, bf16[128,4096]{1,0:T(8,128)(2,1)S(1)}) custom-call(bf16[96,4096]{1,0:T(8,128)(2,1)} %x_ref.1, bf16[128,4096]{1,0:T(8,128)(2,1)} %y_ref.1, f32[1,4096]{1,0:T(1,128)S(1)} %copy-done, s32[1]{0:T(128)S(6)} %copy.7.len_ref, bf16[1,4,4096,768]{3,2,1,0:T(8,128)(2,1)} %w_hbm.1), custom_call_target="tpu_custom_call" | custom-call | tf_op jit(solution)/shard_map/pallas_call | solution.py:393
  63.7 1.5 %shard_map.69 = (bf16[96,4096]{1,0:T(8,128)(2,1)}, bf16[128,4096]{1,0:T(8,128)(2,1)}) custom-call(bf16[96,4096]{1,0:T(8,128)(2,1)S(1)} %get-tuple-element.4.a_ref, bf16[128,4096]{1,0:T(8,128)(2,1)S(1)} %get-tuple-element.5.b_ref), custom_call_target="tpu_custom_call" | custom-call | tf_op jit(solution)/shard_map/pallas_call | solution.py:430
Async XLA Ops:
  1.3 0.7 %copy-start = (f32[1,4096]{1,0:T(1,128)S(1)}, f32[1,4096]{1,0:T(1,128)}, u32[]{:S(2)}) copy-start(f32[1,4096]{1,0:T(1,128)} %gain_ref.1) | copy-start | bytes 49156
